TPU v7x, 32 devices: a whole 2x2x4 slice. The times are simulated.
32 devices in a mesh: dp: 8 (over z, x), tensor: 4 (over y, core).
Axes of the slice: x: 2, y: 2, z: 4, core: 2. Of those that a mesh axis runs over, the one named last changes fastest.
Arguments:
- attn_out: bfloat16 [4096, 2560], P('dp', 'tensor'), may hold values from -6 to 6
- resid: bfloat16 [4096, 5120], P('dp', 'tensor'), may hold values from -6 to 6
- out_proj: bfloat16 [2560, 5120], P('tensor'), may hold values from -0.125 to 0.125
- heads: bfloat16 [5120, 8], P('tensor'), may hold values from -0.078125 to 0.078125
- gain: bfloat16 [5120], P('tensor'), may hold values from 0.25 to 1.75
- lengths: int32 [64], P('dp'), may hold values from 0 to 63
Outputs:
- uwo: float32 [64], P('dp')
- proj_grad: float32 [5120, 2560], P('dp', 'tensor')
- head_grad: float32 [5120, 8], P('tensor')
- gain_grad: float32 [5120], P('tensor')
Inputs may be any that keep to these rules, and one draw needn't show every extreme that they name: Positions 0 to lengths[n] of response n are scored.
All inputs are finite; a program needn't handle non-finite values.
Results may differ from a plain program's by a relative error of at most 0.0085.
Values may be sent and summed in bfloat16 or wider, within the bound.
A program may use at most 128 MiB of HBM per device.

v0:
```python
import jax
import jax.numpy as jnp
from jax import lax
from jax.sharding import PartitionSpec as P

D = 5120
EPS_NORM = 1e-06
EPS_VAR = 1e-05
PENALTY = 0.5


def per_device(attn_out, resid, out_proj, heads, gain, lengths):
    total_rows = attn_out.shape[0]
    resp_dev = lengths.shape[0]
    seq_len = total_rows // resp_dev
    members = heads.shape[1]
    highest = lax.Precision.HIGHEST
    product = jnp.dot(attn_out, out_proj, preferred_element_type=jnp.float32)
    gain_local = gain.astype(jnp.float32)
    heads_local = heads.astype(jnp.float32)
    hidden = resid.astype(jnp.float32) + lax.psum_scatter(
        product.astype(jnp.bfloat16), "tensor", scatter_dimension=1, tiled=True
    ).astype(jnp.float32)
    squares = lax.psum(jnp.sum(hidden * hidden, axis=1), "tensor")
    rinv = lax.rsqrt(squares / D + EPS_NORM)
    normed = hidden * rinv[:, None] * gain_local[None, :]
    scores = lax.psum(jnp.dot(normed, heads_local, precision=highest), "tensor")
    position = lax.broadcasted_iota(jnp.int32, (resp_dev, seq_len), 1)
    inside = position <= lengths[:, None]
    counts = (lengths + 1).astype(jnp.float32)
    per_resp = scores.reshape(resp_dev, seq_len, members)
    rewards = jnp.sum(jnp.where(inside[:, :, None], per_resp, 0.0), axis=1) / counts[:, None]
    total_resp = resp_dev * lax.axis_size("dp")
    first_sum, second_sum = lax.psum(
        (jnp.sum(rewards, axis=0), jnp.sum(rewards * rewards, axis=0)), "dp"
    )
    center = first_sum / total_resp
    spread = second_sum / total_resp - center * center
    zed = (rewards - center[None, :]) * lax.rsqrt(spread + EPS_VAR)[None, :]
    zmean = jnp.mean(zed, axis=1)
    uwo = zmean - PENALTY * jnp.mean((zed - zmean[:, None]) ** 2, axis=1)
    pairs = rewards.reshape(resp_dev // 2, 2, members)
    weight = jax.nn.sigmoid(pairs[:, 1] - pairs[:, 0])
    dreward = jnp.stack([-weight, weight], axis=1).reshape(resp_dev, members)
    dscore = jnp.where(inside[:, :, None], (dreward / counts[:, None])[:, None, :], 0.0).reshape(
        total_rows, members
    )
    dnormed_local = jnp.dot(dscore, heads_local.T, precision=highest)
    inner = lax.psum(jnp.sum(hidden * gain_local[None, :] * dnormed_local, axis=1), "tensor")
    dhidden = (
        rinv[:, None] * gain_local[None, :] * dnormed_local
        - hidden * (rinv**3 * inner / D)[:, None]
    ).astype(jnp.bfloat16)
    head_term = jnp.dot(normed.T, dscore, precision=highest)
    gain_term = jnp.sum(dnormed_local * hidden * rinv[:, None], axis=0)
    head_grad, gain_grad = lax.psum((head_term, gain_term), "dp")
    term = jnp.einsum(
        "rd,rj->dj",
        lax.all_gather(dhidden, "tensor", axis=1, tiled=True),
        attn_out,
        preferred_element_type=jnp.float32,
    )
    proj_grad = lax.psum_scatter(term, "dp", scatter_dimension=0, tiled=True)
    return (uwo, proj_grad, head_grad, gain_grad)


def solution(mesh):
    return jax.shard_map(
        per_device,
        mesh=mesh,
        in_specs=(
            P("dp", "tensor"),
            P("dp", "tensor"),
            P("tensor", None),
            P("tensor", None),
            P("tensor"),
            P("dp"),
        ),
        out_specs=(P("dp"), P("dp", "tensor"), P("tensor", None), P("tensor")),
        check_vma=False,
    )
```

profile of v0, /device:TPU:0, one launch (start us, length us, event | category | flops | bytes accessed | tf_op | source)
XLA Modules:
  0.0 384.5 jit_solution(8206958620141189595)
XLA Ops:
  7.2 0.0 copy-start
  7.2 0.0 reduce-scatter.3.cloned.1.call-start
  7.2 1.0 copy-done
  8.3 8.8 %convolution_convert_fusion = bf16[512,5120]{1,0:T(8,128)(2,1)} fusion(bf16[512,640]{1,0:T(8,128)(2,1)S(1)} %copy-done, bf16[640,5120]{1,0:T(8,128)(2,1)} %param.8), kind=kOutput, calls=%fused_computation | convolution fusion | flops 3358064640 | bytes 12451840 | tf_op jit(solution)/shard_map/dot_general | solution.py:18
  17.1 0.0 copy-start.8
  17.1 0.0 copy-start.6
  17.1 0.0 copy-start.1
  17.1 0.0 reduce-scatter.3.cloned.1.call-update
  17.1 0.0 copy-start.7
  17.1 0.0 all-gather.2.cloned.1.call-start
  17.2 0.6 copy-done.8
  17.7 0.1 iota_compare_fusion
  17.8 0.6 le.18
  18.4 0.0 copy-start.5
  18.4 0.1 div.52
  18.5 0.1 copy.14
  18.6 0.0 copy-done.6
  18.6 52.6 %reduce-scatter.3.cloned.1.call-done = bf16[512,1280]{1,0:T(8,128)(2,1)} async-done(((bf16[512,5120]{1,0:T(8,128)(2,1)}), bf16[512,1280]{1,0:T(8,128)(2,1)}) %reduce-scatter.3.cloned.1.call-update) | async-done | bytes 1310736 | tf_op jit(solution)/shard_map/reduce_scatter | solution.py:21
  71.2 0.0 copy-done.1
  71.2 0.0 copy-start.2
  71.2 1.9 multiply_reduce_fusion.2
  73.1 5.8 %psum.49 = f32[512]{0:T(512)S(1)} all-reduce(f32[512]{0:T(512)S(1)} %multiply_reduce_fusion.2), channel_id=1, replica_groups=mesh['dp'=8,'tensor'=4] {'tensor'}, use_global_device_ids=true, to_apply=%region_2.0 | all-reduce | flops 512 | bytes 4096 | tf_op jit(solution)/shard_map/psum | solution.py:24
  78.9 0.0 copy-done.7
  78.9 0.0 copy-done.2
  78.9 0.0 copy-start.3
  78.9 1.7 fusion.1
  80.6 0.1 reshape.69
  80.7 0.0 copy-done.3
  80.7 10.3 %psum.50 = f32[8,64,8]{1,0,2:T(8,128)S(1)} all-reduce(f32[8,64,8]{1,0,2:T(8,128)S(1)} %reshape.69), channel_id=1, replica_groups=mesh['dp'=8,'tensor'=4] {'tensor'}, use_global_device_ids=true, to_apply=%region_3.0 | all-reduce | flops 4096 | bytes 32768 | tf_op jit(solution)/shard_map/psum | solution.py:27
  91.0 0.1 select_reduce_fusion
  91.0 0.1 copy.13
  91.1 0.1 copy_divide_fusion
  91.2 0.1 copy.17
  91.3 0.0 copy-done.5
  91.3 0.7 fusion.13
  92.0 0.7 copy.18
  92.7 0.8 bitcast_select_fusion
  93.5 4.6 %multiply_reduce_fusion = (f32[1280]{0:T(1024)}, f32[512]{0:T(512)}, f32[512,1280]{1,0:T(8,128)}) fusion(bf16[512,1280]{1,0:T(8,128)(2,1)S(1)} %copy-done.2, bf16[512,1280]{1,0:T(8,128)(2,1)S(1)} %copy-done.1, f32[512]{0:T(512)} %copy-done.3, f32[1280]{0:T(1024)S(1)} %convert_element_type.22, f32[512,8]{1,0:T(8,128)S(1)} %bitcast_select_fusion, ...), kind=kOutput, calls=%fused_computation.1 | convolution fusion | flops 68811008 | bytes 5294080 | tf_op jit(solution)/shard_map/dot_general | solution.py:48
  98.2 6.8 %psum.53 = f32[512]{0:T(512)} all-reduce(f32[512]{0:T(512)} %get-tuple-element.5), channel_id=1, replica_groups=mesh['dp'=8,'tensor'=4] {'tensor'}, use_global_device_ids=true, to_apply=%region_12.13 | all-reduce | flops 512 | bytes 4096 | tf_op jit(solution)/shard_map/psum | solution.py:49
  105.0 0.7 fusion.8
  105.7 3.5 subtract_convert_fusion
  109.2 0.0 all-gather.2.cloned.1.call-update
  109.2 0.2 reduce-scatter.5.cloned.1.call-start
  109.5 40.8 %all-gather.2.cloned.1.call-done = bf16[512,5120]{1,0:T(8,128)(2,1)} async-done(((bf16[512,1280]{1,0:T(8,128)(2,1)}), bf16[512,5120]{1,0:T(8,128)(2,1)}) %all-gather.2.cloned.1.call-update) | async-done | bytes 5242896 | tf_op jit(solution)/shard_map/all_gather | solution.py:59
  150.2 11.4 %fusion.16 = f32[5120,640]{1,0:T(8,128)} fusion(bf16[512,5120]{1,0:T(8,128)(2,1)} %all-gather.2.cloned.1.call-done, bf16[512,640]{1,0:T(8,128)(2,1)S(1)} %copy-done), kind=kOutput, calls=%fused_computation.40 | convolution fusion | flops 3355443200 | bytes 19005440 | tf_op jit(solution)/shard_map/rd,rj->dj/dot_general | solution.py:57
  161.7 0.0 copy-start.4
  161.7 0.0 reduce-scatter.5.cloned.1.call-update
  161.7 0.7 copy-done.4
  162.3 2.5 fusion
  164.9 41.5 %all-reduce = (f32[8]{0:T(128)S(1)}, f32[8]{0:T(128)S(1)}, f32[1280,8]{0,1:T(8,128)}, f32[1280]{0:T(1024)}) all-reduce(f32[8]{0:T(128)} %get-tuple-element.7, f32[8]{0:T(128)} %get-tuple-element.6, f32[1280,8]{0,1:T(8,128)} %fusion, f32[1280]{0:T(1024)} %get-tuple-element.4), channel_id=1, replica_groups=mesh['dp'=8,'tensor'=4] {'dp'}, use_global_device_ids=true, to_apply=%region_8.9 | all-reduce | flops 11536 | bytes 92288 | tf_op jit(solution)/shard_map/psum | solution.py:34
  206.4 0.8 fusion.6
  207.1 0.8 multiply_reduce_fusion.3
  207.9 0.5 multiply_subtract_fusion
  208.4 169.5 %reduce-scatter.5.cloned.1.call-done = f32[640,640]{1,0:T(8,128)} async-done(((f32[5120,640]{1,0:T(8,128)}), f32[640,640]{1,0:T(8,128)}) %reduce-scatter.5.cloned.1.call-update) | async-done | bytes 1638416 | tf_op jit(solution)/shard_map/reduce_scatter | solution.py:63
  (8 shorter events, 0.0 us)
Async XLA Ops:
  7.2 1.1 copy-start
  7.2 64.0 %reduce-scatter.3.cloned.1.call-start = ((), (), s32[]{:S(2)}) async-start(), calls=%async_computation.2 | async-start | bytes 6553600 | tf_op jit(solution)/shard_map/reduce_scatter | solution.py:21
  17.1 0.7 copy-start.8
  17.1 1.5 copy-start.6
  17.1 54.1 %copy-start.1 = (bf16[512,1280]{1,0:T(8,128)(2,1)S(1)}, bf16[512,1280]{1,0:T(8,128)(2,1)}, u32[]{:S(2)}) copy-start(bf16[512,1280]{1,0:T(8,128)(2,1)} %param.7) | copy-start | bytes 3932164
  17.1 61.8 %copy-start.7 = (bf16[1280,8]{0,1:T(8,128)(2,1)S(1)}, bf16[1280,8]{0,1:T(8,128)(2,1)}, u32[]{:S(2)}) copy-start(bf16[1280,8]{0,1:T(8,128)(2,1)} %param.9) | copy-start | bytes 61444
  17.1 133.1 %all-gather.2.cloned.1.call-start = ((), (), s32[]{:S(2)}) async-start(), calls=%async_computation.3 | async-start | bytes 6553600 | tf_op jit(solution)/shard_map/all_gather | solution.py:59
  18.4 72.9 %copy-start.5 = (f32[8]{0:T(128)}, f32[8]{0:T(128)S(1)}, u32[]{:S(2)}) copy-start(f32[8]{0:T(128)S(1)} %add_convert_fusion) | copy-start | bytes 100
  71.2 7.7 %copy-start.2 = (bf16[512,1280]{1,0:T(8,128)(2,1)S(1)}, bf16[512,1280]{1,0:T(8,128)(2,1)}, u32[]{:S(2)}) copy-start(bf16[512,1280]{1,0:T(8,128)(2,1)} %reduce-scatter.3.cloned.1.call-done) | copy-start | bytes 3932164
  78.9 1.8 copy-start.3
  109.2 268.7 %reduce-scatter.5.cloned.1.call-start = ((), (), s32[]{:S(2)}) async-start(), calls=%async_computation.4 | async-start | bytes 14745600 | tf_op jit(solution)/shard_map/reduce_scatter | solution.py:63
  161.7 0.7 copy-start.4
Sparse Core Ops, SparseCore 0:
  17.2 53.8 reduce-scatter.2
  109.4 40.8 all-gather.1
  161.8 216.0 reduce-scatter.4
where the time goes:
time: 385 us; the launch traced here: 384 us
  waiting for transfers between devices  263 us (68%)
  blocking collectives  64.3 us (17%)
  matrix products  29.2 us (8%)
  between operations  13.8 us (4%)
  other arithmetic  9.97 us (3%)
  local copies, waits for them, and re-layouts  3.95 us (1%)
    reduce_scatter x1, waiting for transfers between devices, per_device(): proj_grad = lax.psum_scatter(term, 'dp', scatter_dimension=0, tiled=True)  170 us
    reduce_scatter x1, waiting for transfers between devices, per_device(): lax.psum_scatter(product.astype(jnp.bfloat16), 'tensor', scatter_dimensio...  52.6 us
    psum x1, blocking collectives, per_device(): lax.psum((jnp.sum(rewards, axis=0), jnp.sum(rewards * rewards, axis=0)),...  41.5 us
    all_gather x1, waiting for transfers between devices, per_device(): lax.all_gather(dhidden, 'tensor', axis=1, tiled=True)  40.8 us
    dot_general x1, matrix products, per_device(): jnp.einsum('rd,rj->dj', lax.all_gather(dhidden, 'tensor', axis=1, tiled=T...  11.4 us
    psum x1, blocking collectives, per_device(): scores = lax.psum(jnp.dot(normed, heads_local, precision=highest), 'tensor')  10.3 us
    dot_general x1, matrix products, per_device(): product = jnp.dot(attn_out, out_proj, preferred_element_type=jnp.float32)  8.81 us
  transfers between devices with their start and end apart: 3, of which 3 were waited for; matrix products, arithmetic and copies ran while one was open for 1% of the time, Pallas kernels for 0%

commit v1 on v0

--- a/solution.py
+++ b/solution.py
@@ -54,12 +54,19 @@
     head_term = jnp.dot(normed.T, dscore, precision=highest)
     gain_term = jnp.sum(dnormed_local * hidden * rinv[:, None], axis=0)
     head_grad, gain_grad = lax.psum((head_term, gain_term), "dp")
-    term = jnp.einsum(
-        "rd,rj->dj",
-        lax.all_gather(dhidden, "tensor", axis=1, tiled=True),
-        attn_out,
-        preferred_element_type=jnp.float32,
-    )
+    x = dhidden
+    ways, here, step = (lax.axis_size("tensor"), lax.axis_index("tensor"), x.shape[1])
+    results = []
+    for far in range(ways):
+        arriving = (
+            lax.ppermute(x, "tensor", [(d, (d + 1) % ways) for d in range(ways)])
+            if far + 1 < ways
+            else x
+        )
+        results.append(jnp.einsum("rd,rj->dj", x, attn_out, preferred_element_type=jnp.float32))
+        x = arriving
+    line = jnp.concatenate(results[::-1], axis=0)
+    term = jnp.roll(line, (here + 1) * results[0].shape[0], axis=0)
     proj_grad = lax.psum_scatter(term, "dp", scatter_dimension=0, tiled=True)
     return (uwo, proj_grad, head_grad, gain_grad)
 

time: 385 us -> 416 us (1.081)
  local copies, waits for them, and re-layouts: 3.95 us -> 23.8 us
  waiting for transfers between devices: 263 us -> 273 us
    ppermute x0 -> x3, waiting for transfers between devices: none -> 51.5 us  [per_device(): lax.ppermute(x, 'tensor', [(d, (d + 1) % ways) for d in range(ways)])]
    all_gather x1 -> x0, waiting for transfers between devices: 40.8 us -> none  [per_device(): lax.all_gather(dhidden, 'tensor', axis=1, tiled=True)]
    dynamic_slice x0 -> x1, local copies, waits for them, and re-layouts: none -> 10.5 us  [per_device(): term = jnp.roll(line, (here + 1) * results[0].shape[0], axis=0)]
    unnamed x18 -> x29, local copies, waits for them, and re-layouts: 2.29 us -> 9.76 us
    dot_general x1 -> x4, matrix products: 11.4 us -> 14.5 us  [per_device(): jnp.einsum('rd,rj->dj', x, attn_out, preferred_element_type=jnp.float32)]
  transfers between devices with their start and end apart: 3 -> 5, of which waited for: 3 -> 5; matrix products, arithmetic and copies ran while one was open for 1% -> 1% of each run, Pallas kernels for 0% -> 0%
where the time goes in v1:
time: 416 us
  waiting for transfers between devices  273 us (66%)
  blocking collectives  64 us (15%)
  matrix products  32.1 us (8%)
  local copies, waits for them, and re-layouts  23.8 us (6%)
  between operations  14.2 us (3%)
  other arithmetic  8.57 us (2%)
    reduce_scatter x1, waiting for transfers between devices, per_device(): proj_grad = lax.psum_scatter(term, 'dp', scatter_dimension=0, tiled=True)  169 us
    reduce_scatter x1, waiting for transfers between devices, per_device(): lax.psum_scatter(product.astype(jnp.bfloat16), 'tensor', scatter_dimensio...  52.5 us
    ppermute x3, waiting for transfers between devices, per_device(): lax.ppermute(x, 'tensor', [(d, (d + 1) % ways) for d in range(ways)])  51.5 us
    psum x1, blocking collectives, per_device(): lax.psum((jnp.sum(rewards, axis=0), jnp.sum(rewards * rewards, axis=0)),...  41.7 us
    dot_general x4, matrix products, per_device(): jnp.einsum('rd,rj->dj', x, attn_out, preferred_element_type=jnp.float32)  14.5 us
    dynamic_slice x1, local copies, waits for them, and re-layouts, per_device(): term = jnp.roll(line, (here + 1) * results[0].shape[0], axis=0)  10.5 us
    psum x1, blocking collectives, per_device(): scores = lax.psum(jnp.dot(normed, heads_local, precision=highest), 'tensor')  10.3 us
    unnamed x29, local copies, waits for them, and re-layouts  9.76 us
  transfers between devices with their start and end apart: 5, of which 5 were waited for; matrix products, arithmetic and copies ran while one was open for 1% of the time, Pallas kernels for 0%

profile of v1, /device:TPU:0, one launch (start us, length us, event | category | flops | bytes accessed | tf_op | source)
XLA Modules:
  0.0 415.6 jit_solution(12625820814611946100)
XLA Ops:
  7.2 0.0 copy-start
  7.2 0.0 reduce-scatter.3.cloned.1.call-start
  7.2 1.0 copy-done
  8.3 8.8 %convolution_convert_fusion = bf16[512,5120]{1,0:T(8,128)(2,1)} fusion(bf16[512,640]{1,0:T(8,128)(2,1)S(1)} %copy-done, bf16[640,5120]{1,0:T(8,128)(2,1)} %param.8), kind=kOutput, calls=%fused_computation | convolution fusion | flops 3358064640 | bytes 12451840 | tf_op jit(solution)/shard_map/dot_general | solution.py:18
  17.1 0.0 copy-start.10
  17.1 0.0 reduce-scatter.3.cloned.1.call-update
  17.1 0.0 copy-start.11
  17.1 0.0 reduce-scatter.5.cloned.1.call-start
  17.2 0.6 copy-done.10
  17.8 0.0 copy-done.12
  17.8 0.0 copy-start.9
  17.8 0.1 div.52
  17.9 0.1 copy.14
  18.0 0.1 iota_compare_fusion
  18.0 0.6 le.18
  18.6 52.5 %reduce-scatter.3.cloned.1.call-done = bf16[512,1280]{1,0:T(8,128)(2,1)} async-done(((bf16[512,5120]{1,0:T(8,128)(2,1)}), bf16[512,1280]{1,0:T(8,128)(2,1)}) %reduce-scatter.3.cloned.1.call-update) | async-done | bytes 1310736 | tf_op jit(solution)/shard_map/reduce_scatter | solution.py:21
  71.2 0.0 copy-done.2
  71.2 1.9 multiply_reduce_fusion.2
  73.1 5.8 %psum.49 = f32[512]{0:T(512)S(1)} all-reduce(f32[512]{0:T(512)S(1)} %multiply_reduce_fusion.2), channel_id=1, replica_groups=mesh['dp'=8,'tensor'=4] {'tensor'}, use_global_device_ids=true, to_apply=%region_2.0 | all-reduce | flops 512 | bytes 4096 | tf_op jit(solution)/shard_map/psum | solution.py:24
  78.9 0.0 copy-done.11
  78.9 0.0 copy-done.3
  78.9 0.0 copy-start.7
  78.9 1.7 fusion.1
  80.6 0.1 reshape.69
  80.7 0.0 copy-done.7
  80.7 10.3 %psum.50 = f32[8,64,8]{1,0,2:T(8,128)S(1)} all-reduce(f32[8,64,8]{1,0,2:T(8,128)S(1)} %reshape.69), channel_id=1, replica_groups=mesh['dp'=8,'tensor'=4] {'tensor'}, use_global_device_ids=true, to_apply=%region_3.0 | all-reduce | flops 4096 | bytes 32768 | tf_op jit(solution)/shard_map/psum | solution.py:27
  91.0 0.1 select_reduce_fusion
  91.0 0.1 copy.13
  91.1 0.1 copy_divide_fusion
  91.2 0.1 copy.17
  91.3 0.0 copy-done.9
  91.3 0.7 fusion.13
  92.0 0.7 copy.18
  92.7 0.8 bitcast_select_fusion
  93.5 4.6 %multiply_reduce_fusion = (f32[1280]{0:T(1024)}, f32[512]{0:T(512)}, f32[512,1280]{1,0:T(8,128)}) fusion(bf16[512,1280]{1,0:T(8,128)(2,1)S(1)} %copy-done.3, bf16[512,1280]{1,0:T(8,128)(2,1)S(1)} %copy-done.2, f32[512]{0:T(512)} %copy-done.7, f32[1280]{0:T(1024)S(1)} %convert_element_type.22, f32[512,8]{1,0:T(8,128)S(1)} %bitcast_select_fusion, ...), kind=kOutput, calls=%fused_computation.1 | convolution fusion | flops 68811008 | bytes 5294080 | tf_op jit(solution)/shard_map/dot_general | solution.py:48
  98.1 6.3 %psum.53 = f32[512]{0:T(512)S(1)} all-reduce(f32[512]{0:T(512)} %get-tuple-element.5), channel_id=1, replica_groups=mesh['dp'=8,'tensor'=4] {'tensor'}, use_global_device_ids=true, to_apply=%region_12.13 | all-reduce | flops 512 | bytes 4096 | tf_op jit(solution)/shard_map/psum | solution.py:49
  104.4 2.8 subtract_convert_fusion
  107.2 0.1 collective-permute-start
  107.3 17.0 %collective-permute-done = bf16[512,1280]{1,0:T(8,128)(2,1)S(1)} collective-permute-done((bf16[512,1280]{1,0:T(8,128)(2,1)S(1)}, bf16[512,1280]{1,0:T(8,128)(2,1)S(1)}, u32[]{:S(2)}, u32[]{:S(2)}) %collective-permute-start) | collective-permute-done | bytes 1310752 | tf_op jit(solution)/shard_map/ppermute | solution.py:62
  124.3 1.1 copy-done.5
  125.3 0.0 collective-permute-start.1
  125.3 17.1 %collective-permute-done.1 = bf16[512,1280]{1,0:T(8,128)(2,1)} collective-permute-done((bf16[512,1280]{1,0:T(8,128)(2,1)S(1)}, bf16[512,1280]{1,0:T(8,128)(2,1)}, u32[]{:S(2)}, u32[]{:S(2)}) %collective-permute-start.1) | collective-permute-done | bytes 1310752 | tf_op jit(solution)/shard_map/ppermute | solution.py:62
  142.5 0.0 collective-permute-start.2
  142.5 17.3 %collective-permute-done.2 = bf16[512,1280]{1,0:T(8,128)(2,1)} collective-permute-done((bf16[512,1280]{1,0:T(8,128)(2,1)}, bf16[512,1280]{1,0:T(8,128)(2,1)}, u32[]{:S(2)}, u32[]{:S(2)}) %collective-permute-start.2) | collective-permute-done | bytes 1310752 | tf_op jit(solution)/shard_map/ppermute | solution.py:62
  159.8 4.2 %constant_dynamic-update-slice_fusion.7 = (f32[10240,640]{1,0:T(8,128)}, f32[1280,640]{1,0:T(8,128)S(1)}) fusion(bf16[512,1280]{1,0:T(8,128)(2,1)} %collective-permute-done.2, bf16[512,640]{1,0:T(8,128)(2,1)S(1)} %copy-done), kind=kOutput, calls=%fused_computation.22 | convolution fusion | flops 838860800 | bytes 8519680 | tf_op jit(solution)/shard_map/rd,rj->dj/dot_general | solution.py:66
  164.0 4.4 %constant_dynamic-update-slice_fusion.6 = (f32[10240,640]{1,0:T(8,128)}, f32[1280,640]{1,0:T(8,128)S(1)}) fusion(f32[10240,640]{1,0:T(8,128)} %get-tuple-element.18, bf16[512,1280]{1,0:T(8,128)(2,1)} %collective-permute-done.1, bf16[512,640]{1,0:T(8,128)(2,1)S(1)} %copy-done), kind=kOutput, calls=%fused_computation.21 | convolution fusion | flops 838860800 | bytes 8519680 | tf_op jit(solution)/shard_map/rd,rj->dj/dot_general | solution.py:66
  168.4 0.0 copy-done.6
  168.4 3.0 constant_dynamic-update-slice_fusion.5
  171.4 2.9 constant_dynamic-update-slice_fusion.4
  174.3 1.9 constant_dynamic-update-slice_fusion.3
  176.2 1.9 constant_dynamic-update-slice_fusion.2
  178.1 2.0 constant_dynamic-update-slice_fusion.1
  180.0 1.9 constant_dynamic-update-slice_fusion
  182.0 10.5 %constant_dynamic-slice_fusion = f32[5120,640]{1,0:T(8,128)} fusion(f32[10240,640]{1,0:T(8,128)} %constant_dynamic-update-slice_fusion, s32[]{:T(128)S(6)} %select_n.25), kind=kLoop, calls=%fused_computation.44 | loop fusion | bytes 26214404 | tf_op jit(solution)/shard_map/jit(_roll_dynamic)/dynamic_slice | solution.py:69
  192.5 0.0 reduce-scatter.5.cloned.1.call-update
  192.5 1.3 copy-done.4
  193.8 0.0 copy-done.8
  193.8 2.5 fusion
  196.3 41.7 %all-reduce = (f32[8]{0:T(128)S(1)}, f32[8]{0:T(128)S(1)}, f32[1280,8]{0,1:T(8,128)}, f32[1280]{0:T(1024)}) all-reduce(f32[8]{0:T(128)} %get-tuple-element.7, f32[8]{0:T(128)} %get-tuple-element.6, f32[1280,8]{0,1:T(8,128)} %fusion, f32[1280]{0:T(1024)} %get-tuple-element.4), channel_id=1, replica_groups=mesh['dp'=8,'tensor'=4] {'dp'}, use_global_device_ids=true, to_apply=%region_8.9 | all-reduce | flops 11536 | bytes 92288 | tf_op jit(solution)/shard_map/psum | solution.py:34
  238.0 0.7 fusion.6
  238.7 0.7 multiply_reduce_fusion.3
  239.5 0.5 multiply_subtract_fusion
  240.0 168.7 %reduce-scatter.5.cloned.1.call-done = f32[640,640]{1,0:T(8,128)} async-done(((f32[5120,640]{1,0:T(8,128)}), f32[640,640]{1,0:T(8,128)}) %reduce-scatter.5.cloned.1.call-update) | async-done | bytes 1638416 | tf_op jit(solution)/shard_map/reduce_scatter | solution.py:70
  408.8 0.0 copy-done.1
  (17 shorter events, 0.1 us)
Async XLA Ops:
  7.2 1.1 copy-start
  7.2 64.0 %reduce-scatter.3.cloned.1.call-start = ((), (), s32[]{:S(2)}) async-start(), calls=%async_computation.2 | async-start | bytes 6553600 | tf_op jit(solution)/shard_map/reduce_scatter | solution.py:21
  17.1 0.7 copy-start.10
  17.1 0.7 copy-start.12
  17.1 54.1 %copy-start.2 = (bf16[512,1280]{1,0:T(8,128)(2,1)S(1)}, bf16[512,1280]{1,0:T(8,128)(2,1)}, u32[]{:S(2)}) copy-start(bf16[512,1280]{1,0:T(8,128)(2,1)} %param.7) | copy-start | bytes 3932164
  17.1 61.8 %copy-start.11 = (bf16[1280,8]{0,1:T(8,128)(2,1)S(1)}, bf16[1280,8]{0,1:T(8,128)(2,1)}, u32[]{:S(2)}) copy-start(bf16[1280,8]{0,1:T(8,128)(2,1)} %param.9) | copy-start | bytes 61444
  17.1 391.6 %reduce-scatter.5.cloned.1.call-start = ((), (), s32[]{:S(2)}) async-start(), calls=%async_computation.3 | async-start | bytes 14745600 | tf_op jit(solution)/shard_map/reduce_scatter | solution.py:70
  17.8 73.5 %copy-start.9 = (f32[8]{0:T(128)}, f32[8]{0:T(128)S(1)}, u32[]{:S(2)}) copy-start(f32[8]{0:T(128)S(1)} %add_convert_fusion) | copy-start | bytes 100
  71.2 7.7 %copy-start.3 = (bf16[512,1280]{1,0:T(8,128)(2,1)S(1)}, bf16[512,1280]{1,0:T(8,128)(2,1)}, u32[]{:S(2)}) copy-start(bf16[512,1280]{1,0:T(8,128)(2,1)} %reduce-scatter.3.cloned.1.call-done) | copy-start | bytes 3932164
  78.9 1.8 copy-start.7
  107.2 17.1 %collective-permute-start = (bf16[512,1280]{1,0:T(8,128)(2,1)S(1)}, bf16[512,1280]{1,0:T(8,128)(2,1)S(1)}, u32[]{:S(2)}, u32[]{:S(2)}) collective-permute-start(bf16[512,1280]{1,0:T(8,128)(2,1)S(1)} %subtract_convert_fusion), channel_id=1, source_target_pairs={{0,1},{1,2},{2,3},{3,0},{4,5},{5,6},{6,7},{7,4},{8,9},{9,10},{10,1... | collective-permute-start | bytes 3932168 | tf_op jit(solution)/shard_map/ppermute | solution.py:62
  124.3 1.1 copy-start.5
  125.3 17.1 %collective-permute-start.1 = (bf16[512,1280]{1,0:T(8,128)(2,1)S(1)}, bf16[512,1280]{1,0:T(8,128)(2,1)}, u32[]{:S(2)}, u32[]{:S(2)}) collective-permute-start(bf16[512,1280]{1,0:T(8,128)(2,1)S(1)} %collective-permute-done), channel_id=1, source_target_pairs={{0,1},{1,2},{2,3},{3,0},{4,5},{5,6},{6,7},{7,4},{8,9},{9,10},{10,1... | collective-permute-start | bytes 3932168 | tf_op jit(solution)/shard_map/ppermute | solution.py:62
  142.5 17.3 %collective-permute-start.2 = (bf16[512,1280]{1,0:T(8,128)(2,1)}, bf16[512,1280]{1,0:T(8,128)(2,1)}, u32[]{:S(2)}, u32[]{:S(2)}) collective-permute-start(bf16[512,1280]{1,0:T(8,128)(2,1)} %collective-permute-done.1), channel_id=1, source_target_pairs={{0,1},{1,2},{2,3},{3,0},{4,5},{5,6},{6,7},{7,4},{8,9},{9,10},{10,1... | collective-permute-start | bytes 3932168 | tf_op jit(solution)/shard_map/ppermute | solution.py:62
  164.0 4.4 %copy-start.6 = (bf16[512,1280]{1,0:T(8,128)(2,1)S(1)}, bf16[512,1280]{1,0:T(8,128)(2,1)}, u32[]{:S(2)}) copy-start(bf16[512,1280]{1,0:T(8,128)(2,1)} %copy-done.5) | copy-start | bytes 3932164
  192.5 1.3 copy-start.4
  192.5 1.3 copy-start.8
  193.8 215.0 %copy-start.1 = (bf16[512,640]{1,0:T(8,128)(2,1)S(1)}, bf16[512,640]{1,0:T(8,128)(2,1)}, u32[]{:S(2)}) copy-start(bf16[512,640]{1,0:T(8,128)(2,1)} %param.6) | copy-start | bytes 1966084
Sparse Core Ops, SparseCore 0:
  17.2 53.8 reduce-scatter.2
  192.6 216.0 reduce-scatter.4
